TPU v7x, 32 devices: a whole 2x2x4 slice. The times are simulated.
32 devices in a mesh: parts: 2 (over y), mem: 4 (over z), space: 4 (over x, core).
Axes of the slice: x: 2, y: 2, z: 4, core: 2. Of those that a mesh axis runs over, the one named last changes fastest.
Arguments:
- ensemble: bfloat16 [64, 70, 8192], P('mem', None, ('parts', 'space')), parts along dimension 2, may hold values from -6 to 6
- transform: bfloat16 [128, 64], P('parts'), parts along dimension 0, may hold values from -0.75 to 0.75
- obs_operator: bfloat16 [16, 70], replicated, may hold values from -0.75 to 0.75
- obs_weight: float32 [16, 8192], P(None, ('parts', 'space')), parts along dimension 1, may hold values from 0.25 to 40, as said below
Outputs:
- analysis: bfloat16 [64, 70, 8192], P('mem', None, ('parts', 'space')), parts along dimension 2
- prior_gram: float32 [128, 64], P('parts'), parts along dimension 0
- posterior_gram: float32 [128, 64], P('parts'), parts along dimension 0
There are 2 independent parts, one for each index of `parts`. A program takes and returns all parts, laid end to end along the dimension named above; an argument that names none is the same for every part. Nothing has to cross between parts.
Inputs may be any that keep to these rules, and one draw needn't show every extreme that they name: `obs_weight`: positive.
All inputs are finite; a program needn't handle non-finite values.
Results may differ from a plain program's by a relative error of at most 0.001.
Values may be sent and summed in bfloat16 or wider, within the bound.
A program may use at most 64 MiB of HBM per device.

v0:
```python
import functools

import jax
import jax.numpy as jnp
from jax import lax
from jax.experimental import pallas as pl
from jax.experimental.pallas import tpu as pltpu
from jax.sharding import PartitionSpec as P

HIGHEST = lax.Precision.HIGHEST
MESH = pl.DeviceIdType.MESH
LANES = 128
PIECE = 14
ROWS = 16
NT = (((1,), (1,)), ((), ()))


def dot(a, b):
    return jnp.dot(a, b, preferred_element_type=jnp.float32)


def selector(shape, match):
    rows = lax.broadcasted_iota(jnp.int32, shape, 0)
    cols = lax.broadcasted_iota(jnp.int32, shape, 1)
    return match(rows, cols)


def as_bf16(mask):
    return jnp.where(mask, 1.0, 0.0).astype(jnp.bfloat16)


def peers_of(me, size):
    if size % 2:
        return [lax.rem(me + step, size) for step in range(1, size)], []
    half = size // 2
    side, place = me // half, lax.rem(me, half)
    across = [(1 - side) * half + lax.rem(place + step, half) for step in range(half)]
    return across, [side * half + lax.rem(place + step, half) for step in range(1, half)]


def when(needed, condition, body):
    if needed:
        pl.when(condition)(body)
    else:
        body()


def kernel(
    sizes, ensemble, *refs,
):
    smalls, refs = refs[:3], refs[3:]
    analysis, prior, posterior, transform, obs_operator, obs_weight, small_sem = refs[:7]
    (
    arrived, results, observer, observed, gram, by_space, by_mem, in_slabs, out_slabs,
    in_send, in_recv, out_send, out_recv, own_in, own_out,
    space_send, space_recv, mem_send, mem_recv,
    ) = refs[7:]
    n_mem, n_space, active, pieces, local, members, variables, n_obs, chunk = sizes
    blocks = members // ROWS
    aligned = local % ROWS == 0
    partial_owners = active < n_mem
    me = lax.axis_index("mem")
    here = lax.axis_index("space")
    across, beside = peers_of(me, n_mem)
    mem_peers = across + beside
    space_peers = sum(peers_of(here, n_space), [])
    central = jnp.logical_or(me * 2 == n_mem, (me + 1) * 2 == n_mem)

    def lanes_of(owner):
        return pl.ds(pl.multiple_of(owner * chunk, chunk), chunk)

    def rows_of(device):
        return pl.ds(pl.multiple_of(device * local, local), local)

    barrier = pltpu.get_barrier_semaphore()
    for peer in mem_peers:
        pl.semaphore_signal(barrier, inc=1, device_id={"mem": peer}, device_id_type=MESH)
    for peer in space_peers:
        pl.semaphore_signal(barrier, inc=1, device_id={"space": peer}, device_id_type=MESH)
    pl.semaphore_wait(barrier, n_mem - 1 + n_space - 1)

    def spot(whole, slabs, piece, device):
        start, count = pieces[piece]
        if aligned:
            return whole.at[start : start + count, rows_of(device), :]
        return slabs.at[device, start : start + count]

    def outside(array, piece, owner):
        start, count = pieces[piece]
        return array.at[start : start + count, :, lanes_of(owner)]

    def inward(piece, peer, source):
        return pltpu.make_async_remote_copy(
            src_ref=outside(ensemble, piece, peer),
            dst_ref=spot(arrived, in_slabs, piece, source),
            send_sem=in_send.at[piece, peer],
            recv_sem=in_recv.at[piece, source],
            device_id={"mem": peer},
            device_id_type=MESH,
        )

    def inward_own(piece):
        return pltpu.make_async_copy(
            outside(ensemble, piece, me), spot(arrived, in_slabs, piece, me), own_in.at[piece]
        )

    def outward(piece, peer, owner):
        return pltpu.make_async_remote_copy(
            src_ref=spot(results, out_slabs, piece, peer),
            dst_ref=outside(analysis, piece, owner),
            send_sem=out_send.at[piece, peer],
            recv_sem=out_recv.at[piece, owner],
            device_id={"mem": peer},
            device_id_type=MESH,
        )

    def outward_own(piece):
        return pltpu.make_async_copy(
            spot(results, out_slabs, piece, me), outside(analysis, piece, me), own_out.at[piece]
        )

    owns = me < active
    for group in (beside, across):
        for piece in range(len(pieces)):
            for peer in group:
                when(partial_owners, peer < active, lambda: inward(piece, peer, me).start())
    for piece in range(len(pieces)):
        when(partial_owners, owns, lambda: inward_own(piece).start())
    loads = [
        pltpu.make_async_copy(source, target, small_sem.at[index])
        for index, (source, target) in enumerate(
            zip(smalls, (transform, obs_operator, obs_weight))
        )
    ]
    for load in loads:
        load.start()
    for load in loads:
        load.wait()

    eye = as_bf16(selector((members, members), lambda r, c: r == c))
    mixing_t = lax.dot_general(eye, transform[...], NT, preferred_element_type=jnp.float32)
    keep = 1.0 - jnp.sum(mixing_t, axis=1, keepdims=True)
    ones = jnp.ones((ROWS, members), jnp.float32)
    mixer = jnp.concatenate([mixing_t, ones], axis=0).astype(jnp.bfloat16)

    obs_rows = n_obs * ROWS
    obs_pick = as_bf16(selector((obs_rows, n_obs), lambda r, c: r // ROWS == c))
    for piece, (start, count) in enumerate(pieces):
        depth = count * ROWS
        place = as_bf16(selector((variables, depth), lambda r, c: r == c // ROWS + start))
        part = dot(obs_operator[...], place).astype(jnp.bfloat16)
        mask = selector((obs_rows, depth), lambda r, c: lax.rem(r, ROWS) == lax.rem(c, ROWS))
        full = jnp.where(mask, dot(obs_pick, part), 0.0)
        observer[piece, :, 0:depth] = full.astype(jnp.bfloat16)

    def mix(piece):
        start, count = pieces[piece]
        for variable in range(start, start + count):
            if not aligned:
                for device in range(n_mem):
                    rows = slice(device * local, (device + 1) * local)
                    arrived[variable, rows, :] = in_slabs[device, variable]
            mixed = dot(mixer, arrived[variable])
            mean = mixed[members : members + 1, :] / members
            value = (mixed[:members, :] + keep * mean).astype(jnp.bfloat16)
            if aligned:
                results[variable] = value
            else:
                for device in range(n_mem):
                    rows = slice(device * local, (device + 1) * local)
                    out_slabs[device, variable] = value[rows, :]

    def observe(piece):
        start, count = pieces[piece]
        depth = count * ROWS
        for block in range(blocks):
            at = slice(block * ROWS, (block + 1) * ROWS)
            states = arrived[start : start + count, at, :].reshape(depth, chunk)
            term = dot(observer[piece, :, 0:depth], states).reshape(n_obs, ROWS, chunk)
            if piece == 0:
                observed[:, at, :] = term
            else:
                observed[:, at, :] += term

    def form_gram():
        weights = obs_weight[:, lanes_of(me)]
        total = jnp.zeros((members, members), jnp.float32)
        for quantity in range(n_obs):
            values = observed[quantity]
            departures = values - jnp.sum(values, axis=0, keepdims=True) / members
            total += lax.dot_general(
                departures * weights[quantity : quantity + 1, :],
                departures,
                NT,
                precision=HIGHEST,
                preferred_element_type=jnp.float32,
            )
        gram[0:members, 0:members] = total
        gram[members : members + 8, :] = jnp.full((8, LANES), jnp.sum(weights), jnp.float32)

    gram[...] = jnp.zeros_like(gram)

    last = len(pieces) - 1

    def send_back(piece, group):
        for peer in group:
            outward(piece, peer, me).start()

    def work():
        for piece in range(last + 1):
            for peer in mem_peers:
                inward(piece, me, peer).wait_recv()
            inward_own(piece).wait()
            mix(piece)
            send_back(piece, beside)
            if piece < last:
                pl.when(central)(lambda: send_back(piece, across))
            outward_own(piece).start()
            observe(piece)
        form_gram()

    def finish_sends():
        for piece in range(last):
            pl.when(jnp.logical_not(central))(lambda: send_back(piece, across))
        send_back(last, across)

    when(partial_owners, owns, work)

    def exchange(source, slots, index, peers, axis, send, recv, between):
        slots[index] = source
        copies = [
            pltpu.make_async_remote_copy(
                src_ref=slots.at[index],
                dst_ref=slots.at[index],
                send_sem=send.at[peer],
                recv_sem=recv.at[index],
                device_id={axis: peer},
                device_id_type=MESH,
            )
            for peer in peers
        ]
        for copy in copies:
            copy.start()
        between()
        for peer in peers:
            pltpu.make_async_remote_copy(
                src_ref=slots.at[peer],
                dst_ref=slots.at[peer],
                send_sem=send.at[peer],
                recv_sem=recv.at[peer],
                device_id={axis: peer},
                device_id_type=MESH,
            ).wait_recv()
        total = slots[0]
        for slot in range(1, slots.shape[0]):
            total += slots[slot]
        for copy in copies:
            copy.wait_send()
        return total

    total = exchange(
        gram[...], by_space, here, space_peers, "space", space_send, space_recv, lambda: None
    )
    total = exchange(
        total, by_mem, me, mem_peers, "mem", mem_send, mem_recv,
        lambda: when(partial_owners, owns, finish_sends),
    )
    prior_gram = total[0:members, 0:members] / total[members : members + 1, 0:members]
    prior[...] = prior_gram
    carried = jnp.dot(
        mixing_t, prior_gram, precision=HIGHEST, preferred_element_type=jnp.float32
    )
    posterior[...] = jnp.dot(
        carried,
        transform[...].astype(jnp.float32),
        precision=HIGHEST,
        preferred_element_type=jnp.float32,
    )

    for piece in range(len(pieces)):
        for peer in mem_peers:
            when(partial_owners, peer < active, lambda: inward(piece, peer, me).wait_send())
            when(partial_owners, owns, lambda: outward(piece, peer, me).wait_send())
            when(partial_owners, peer < active, lambda: outward(piece, me, peer).wait_recv())
        when(partial_owners, owns, lambda: outward_own(piece).wait())


def store(*refs):
    count = len(refs) // 2
    sources, targets, sems = refs[:count], refs[count : 2 * count], refs[-1]
    pairs = []
    for source, target in zip(sources, targets):
        if len(source.shape) == 3:
            for start in range(0, source.shape[0], PIECE):
                part = slice(start, min(start + PIECE, source.shape[0]))
                pairs.append((source.at[part], target.at[part]))
        else:
            pairs.append((source, target))
    copies = [
        pltpu.make_async_copy(source, target, sems.at[index])
        for index, (source, target) in enumerate(pairs)
    ]
    for copy in copies:
        copy.start()
    for copy in copies:
        copy.wait()


def write_out(*arrays):
    return pl.pallas_call(
        store,
        out_shape=tuple(jax.ShapeDtypeStruct(a.shape, a.dtype) for a in arrays),
        in_specs=[pl.BlockSpec(memory_space=pl.ANY)] * len(arrays),
        out_specs=tuple([pl.BlockSpec(memory_space=pl.ANY)] * len(arrays)),
        scratch_shapes=[pltpu.SemaphoreType.DMA((len(arrays) + pl.cdiv(arrays[0].shape[0], PIECE),))],
        compiler_params=pltpu.CompilerParams(vmem_limit_bytes=8 << 20),
        name="store_outputs",
    )(*arrays)


def per_device(n_mem, n_space, ensemble, transform, obs_operator, obs_weight):
    local, variables, cells = ensemble.shape
    members = transform.shape[0]
    n_obs = obs_operator.shape[0]
    active = min(n_mem, cells // LANES)
    chunk = cells // active
    pieces = tuple(
        (start, min(PIECE, variables - start)) for start in range(0, variables, PIECE)
    )
    sizes = (n_mem, n_space, active, pieces, local, members, variables, n_obs, chunk)
    vmem = pl.BlockSpec(memory_space=pltpu.VMEM)
    any_space = pl.BlockSpec(memory_space=pl.ANY)
    gram_shape = (members + 8, LANES)
    slabs = (1, 1, ROWS, LANES) if local % ROWS == 0 else (n_mem, variables, local, chunk)
    dma = pltpu.SemaphoreType.DMA
    by_variable, prior, posterior = pl.pallas_call(
        functools.partial(kernel, sizes),
        out_shape=(
            pltpu.VMEM((variables, local, cells), jnp.bfloat16),
            pltpu.VMEM((members, members), jnp.float32),
            pltpu.VMEM((members, members), jnp.float32),
        ),
        in_specs=[any_space] * 4,
        out_specs=(vmem, vmem, vmem),
        scratch_shapes=[
            pltpu.VMEM(transform.shape, jnp.bfloat16),
            pltpu.VMEM(obs_operator.shape, jnp.bfloat16),
            pltpu.VMEM(obs_weight.shape, jnp.float32),
            dma((3,)),
            pltpu.VMEM((variables, members, chunk), jnp.bfloat16),
            pltpu.VMEM((variables, members, chunk), jnp.bfloat16),
            pltpu.VMEM((len(pieces), n_obs * ROWS, PIECE * ROWS), jnp.bfloat16),
            pltpu.VMEM((n_obs, members, chunk), jnp.float32),
            pltpu.VMEM(gram_shape, jnp.float32),
            pltpu.VMEM((n_space,) + gram_shape, jnp.float32),
            pltpu.VMEM((n_mem,) + gram_shape, jnp.float32),
            pltpu.VMEM(slabs, jnp.bfloat16),
            pltpu.VMEM(slabs, jnp.bfloat16),
            dma((len(pieces), n_mem)),
            dma((len(pieces), n_mem)),
            dma((len(pieces), n_mem)),
            dma((len(pieces), n_mem)),
            dma((len(pieces),)),
            dma((len(pieces),)),
            dma((n_space,)),
            dma((n_space,)),
            dma((n_mem,)),
            dma((n_mem,)),
        ],
        compiler_params=pltpu.CompilerParams(collective_id=0, has_side_effects=True),
        name="ensemble_exchange",
    )(jnp.transpose(ensemble, (1, 0, 2)), transform, obs_operator, obs_weight)
    by_variable, prior, posterior = write_out(by_variable, prior, posterior)
    return jnp.transpose(by_variable, (1, 0, 2)), prior, posterior


def solution(mesh):
    return jax.shard_map(
        functools.partial(per_device, mesh.shape["mem"], mesh.shape["space"]),
        mesh=mesh,
        in_specs=(
            P("mem", None, ("parts", "space")),
            P("parts", None),
            P(),
            P(None, ("parts", "space")),
        ),
        out_specs=(P("mem", None, ("parts", "space")), P("parts", None), P("parts", None)),
        check_vma=False,
    )
```

profile of v0, /device:TPU:10, one launch (start us, length us, event | category | flops | bytes accessed | tf_op | source)
XLA Modules:
  0.0 108.6 jit_solution(10464401679022857413)
XLA Ops:
  0.6 106.5 %ensemble_exchange.1 = (bf16[70,16,1024]{2,1,0:T(8,128)(2,1)S(1)}, f32[64,64]{1,0:T(8,128)S(1)}, f32[64,64]{1,0:T(8,128)S(1)}) custom-call(bf16[70,16,1024]{2,1,0:T(8,128)(2,1)} %bitcast.2, bf16[64,64]{1,0:T(8,128)(2,1)} %refs_0_.1, bf16[16,70]{1,0:T(8,128)(2,1)} %refs_1_.1, f32[16,1024]{1,0:T(8,128)} %refs_2_.1), custom_call_target="tpu_custom_call" | custom-call | tf_op jit(solution)/shard_map/ensemble_exchange/pallas_call | solution.py:336
  107.2 1.5 %store_outputs.1 = (bf16[70,16,1024]{2,1,0:T(8,128)(2,1)}, f32[64,64]{1,0:T(8,128)}, f32[64,64]{1,0:T(8,128)}) custom-call(bf16[70,16,1024]{2,1,0:T(8,128)(2,1)S(1)} %get-tuple-element.9.refs_0_, f32[64,64]{1,0:T(8,128)S(1)} %get-tuple-element.10.refs_1_, f32[64,64]{1,0:T(8,128)S(1)} %get-tuple-element.11.refs_2_), custom_call_target="tpu_custom_call" | custom-call | tf_op jit(solution)/shard_map/store_outputs/pallas_call | solution.py:310
where the time goes:
time: 110 us; the launch traced here: 109 us
  Pallas kernels  108 us (98%)
    pallas_call x1, Pallas kernels, per_device(): pl.pallas_call(functools.partial(kernel, sizes), out_shape=(pltpu.VMEM((v...  107 us

commit v1 on v0

--- a/solution.py
+++ b/solution.py
@@ -12,6 +12,7 @@
 LANES = 128
 PIECE = 14
 ROWS = 16
+LEAD = 2
 NT = (((1,), (1,)), ((), ()))
 
 
@@ -45,7 +46,7 @@
         body()
 
 
-def kernel(
+def line_kernel(
     sizes, ensemble, *refs,
 ):
     smalls, refs = refs[:3], refs[3:]
@@ -285,6 +286,365 @@
         when(partial_owners, owns, lambda: outward_own(piece).wait())
 
 
+def hub_kernel(
+    sizes, ensemble, transform_in, operator_in, weight_in, analysis, prior, posterior,
+    transform, obs_operator, obs_weight, small_sem,
+    arrived, relay, results, observer, observed, gram, parts, summed, crossed, totals,
+    own_in, end_send, end_recv, relay_send, relay_recv, raw_send, raw_recv,
+    forward_send, forward_recv, beside_send, far_send, near_send, out_recv, near_recv,
+    part_send, part_recv, cross_send, cross_recv, total_send, total_recv, last_send, last_recv,
+    met, ready,
+):
+    n_mem, n_space, pieces, local, members, variables, n_obs, half = sizes
+    blocks = members // ROWS
+    quarter = members // n_space
+    me = lax.axis_index("mem")
+    here = lax.axis_index("space")
+    side = me // (n_mem // 2)
+    is_hub = jnp.logical_or(me * 2 == n_mem, (me + 1) * 2 == n_mem)
+    is_end = jnp.logical_not(is_hub)
+    last_mem = n_mem - 1
+    own_hub, far_hub = 1 + side, 2 - side
+    own_end, far_end = last_mem * side, last_mem - last_mem * side
+    space_peers = [lax.rem(here + step, n_space) for step in range(1, n_space)]
+    order = range(len(pieces))
+
+    def lanes_of(which):
+        return pl.ds(pl.multiple_of(which * half, half), half)
+
+    def rows_of(device):
+        return pl.ds(pl.multiple_of(device * local, local), local)
+
+    def quarter_of(device):
+        return pl.ds(pl.multiple_of(device * quarter, quarter), quarter)
+
+    def signal(sem, **device):
+        pl.semaphore_signal(sem, inc=1, device_id=device, device_id_type=MESH)
+
+    def remote(source, target, send, recv, **device):
+        return pltpu.make_async_remote_copy(
+            src_ref=source, dst_ref=target, send_sem=send, recv_sem=recv,
+            device_id=device, device_id_type=MESH,
+        )
+
+    def span(piece):
+        start, count = pieces[piece]
+        return slice(start, start + count)
+
+    def raw(piece, rows_device, lanes_side):
+        return remote(
+            ensemble.at[span(piece), :, lanes_of(lanes_side)],
+            arrived.at[span(piece), rows_of(rows_device), :],
+            raw_send.at[piece], raw_recv.at[piece], mem=far_hub,
+        )
+
+    def forward(piece, rows_device):
+        return remote(
+            relay.at[span(piece)], arrived.at[span(piece), rows_of(rows_device), :],
+            forward_send.at[piece], forward_recv.at[piece], mem=far_hub,
+        )
+
+    def to_hub(piece):
+        return remote(
+            ensemble.at[span(piece), :, lanes_of(side)],
+            arrived.at[span(piece), rows_of(own_end), :],
+            end_send.at[piece], end_recv.at[piece], mem=own_hub,
+        )
+
+    def to_relay(piece):
+        return remote(
+            ensemble.at[span(piece), :, lanes_of(1 - side)], relay.at[span(piece)],
+            relay_send.at[piece], relay_recv.at[piece], mem=own_hub,
+        )
+
+    def own_raw(piece):
+        return pltpu.make_async_copy(
+            ensemble.at[span(piece), :, lanes_of(side)],
+            arrived.at[span(piece), rows_of(me), :],
+            own_in.at[piece],
+        )
+
+    def outward(block, piece, send, recv, peer, columns):
+        return remote(
+            results.at[span(piece), block * local : (block + 1) * local, :],
+            analysis.at[span(piece), :, lanes_of(columns)],
+            send.at[piece], recv, mem=peer,
+        )
+
+    def to_beside(piece):
+        return outward(0, piece, beside_send, out_recv.at[piece, side], own_end, side)
+
+    def to_near(piece):
+        return outward(1, piece, near_send, near_recv.at[piece], far_hub, side)
+
+    def to_far(piece):
+        return outward(2, piece, far_send, out_recv.at[piece, side], far_end, side)
+
+    def from_side(piece, source):
+        return outward(0, piece, beside_send, out_recv.at[piece, source], own_hub, source)
+
+    loads = [
+        pltpu.make_async_copy(source, target, small_sem.at[index])
+        for index, (source, target) in enumerate(
+            zip((transform_in, operator_in, weight_in), (transform, obs_operator, obs_weight))
+        )
+    ]
+    barrier = pltpu.get_barrier_semaphore()
+
+    @pl.when(is_hub)
+    def _():
+        signal(barrier, mem=far_hub)
+        signal(barrier, mem=own_end)
+        signal(barrier, mem=far_end)
+        pl.semaphore_wait(barrier, 1)
+        for piece in range(LEAD):
+            raw(piece, me, 1 - side).start()
+        for piece in order:
+            own_raw(piece).start()
+
+    @pl.when(is_end)
+    def _():
+        for peer in space_peers:
+            signal(barrier, space=peer)
+        pl.semaphore_wait(barrier, 2 + n_space - 1)
+        to_relay(0).start()
+        for piece in order:
+            if piece + 1 < len(pieces):
+                to_relay(piece + 1).start()
+            to_hub(piece).start()
+        for peer in space_peers:
+            signal(met, space=peer)
+        pl.semaphore_wait(met, n_space - 1)
+        signal(ready, mem=own_hub)
+        signal(ready, mem=far_hub)
+
+    for load in loads:
+        load.start()
+    for load in loads:
+        load.wait()
+    eye = as_bf16(selector((members, members), lambda r, c: r == c))
+    mixing_t = lax.dot_general(eye, transform[...], NT, preferred_element_type=jnp.float32)
+
+    def device_of(block):
+        outer = jnp.where(block == 1, own_end, far_end)
+        inner = jnp.where(block == 0, own_hub, far_hub)
+        return jnp.where(jnp.logical_or(block == 0, block == 2), inner, outer)
+
+    def work():
+        placed = as_bf16(selector(
+            (members, members), lambda r, c: c == device_of(r // local) * local + lax.rem(r, local)
+        ))
+        ordered = lax.dot_general(placed, transform[...], NT, preferred_element_type=jnp.float32)
+        keep = 1.0 - jnp.sum(ordered, axis=1, keepdims=True)
+        ones = jnp.ones((ROWS, members), jnp.float32)
+        mixer = jnp.concatenate([ordered, ones], axis=0).astype(jnp.bfloat16)
+
+        obs_rows = n_obs * ROWS
+        obs_pick = as_bf16(selector((obs_rows, n_obs), lambda r, c: r // ROWS == c))
+        for piece, (start, count) in enumerate(pieces):
+            depth = count * ROWS
+            place = as_bf16(selector((variables, depth), lambda r, c: r == c // ROWS + start))
+            part = dot(obs_operator[...], place).astype(jnp.bfloat16)
+            mask = selector((obs_rows, depth), lambda r, c: lax.rem(r, ROWS) == lax.rem(c, ROWS))
+            full = jnp.where(mask, dot(obs_pick, part), 0.0)
+            observer[piece, :, 0:depth] = full.astype(jnp.bfloat16)
+
+        def feed(piece):
+            to_relay(piece).wait_recv()
+            forward(piece, own_end).start()
+            if piece + LEAD < len(pieces):
+                raw(piece + LEAD, me, 1 - side).start()
+
+        def take(piece):
+            own_raw(piece).wait()
+            to_hub(piece).wait_recv()
+            raw(piece, far_hub, side).wait_recv()
+            forward(piece, far_end).wait_recv()
+
+        def mix(piece):
+            start, count = pieces[piece]
+            for variable in range(start, start + count):
+                mixed = dot(mixer, arrived[variable])
+                mean = mixed[members : members + 1, :] / members
+                value = (mixed[:members, :] + keep * mean).astype(jnp.bfloat16)
+                analysis[variable, :, lanes_of(side)] = value[0:local, :]
+                results[variable] = value[local:, :]
+
+        def observe(piece):
+            start, count = pieces[piece]
+            depth = count * ROWS
+            for block in range(blocks):
+                at = slice(block * ROWS, (block + 1) * ROWS)
+                states = arrived[start : start + count, at, :].reshape(depth, half)
+                term = dot(observer[piece, :, 0:depth], states).reshape(n_obs, ROWS, half)
+                if piece == 0:
+                    observed[:, at, :] = term
+                else:
+                    observed[:, at, :] += term
+
+        def form_gram():
+            weights = obs_weight[:, lanes_of(side)]
+            total = jnp.zeros((members, members), jnp.float32)
+            for quantity in range(n_obs):
+                values = observed[quantity]
+                departures = values - jnp.sum(values, axis=0, keepdims=True) / members
+                total += lax.dot_general(
+                    departures * weights[quantity : quantity + 1, :],
+                    departures,
+                    NT,
+                    precision=HIGHEST,
+                    preferred_element_type=jnp.float32,
+                )
+            gram[...] = jnp.full(gram.shape, jnp.sum(weights), jnp.float32)
+            gram[:, 0:members] = total
+
+        def to_part(peer, slot):
+            return remote(
+                gram.at[quarter_of(peer)], parts.at[slot],
+                part_send.at[peer], part_recv.at[slot], space=peer,
+            )
+
+        def to_cross():
+            return remote(summed, crossed, cross_send.at[0], cross_recv.at[0], mem=far_hub)
+
+        def to_total(peer, source):
+            return remote(
+                totals.at[quarter_of(source)], totals.at[quarter_of(source)],
+                total_send.at[peer], total_recv.at[source], space=peer,
+            )
+
+        steps = len(pieces)
+        for piece in range(min(LEAD, steps)):
+            feed(piece)
+        fed = min(LEAD, steps)
+        pl.semaphore_wait(ready, 2)
+        behind = []
+        for piece in order:
+            take(piece)
+            mix(piece)
+            to_beside(piece).start()
+            behind.append(piece)
+            if fed < steps:
+                feed(fed)
+                fed += 1
+            if fed == steps:
+                for ahead in behind:
+                    to_far(ahead).start()
+                behind = []
+            observe(piece)
+        for piece in range(min(1, steps)):
+            to_near(piece).start()
+        form_gram()
+        for peer in space_peers:
+            to_part(peer, here).start()
+        parts[here] = gram[quarter_of(here), :]
+        for peer in space_peers:
+            to_part(peer, peer).wait_recv()
+        total = parts[0]
+        for slot in range(1, n_space):
+            total += parts[slot]
+        summed[...] = total
+        to_cross().start()
+        for piece in range(min(1, steps), steps):
+            to_near(piece).start()
+        to_cross().wait_recv()
+        totals[quarter_of(here), :] = total + crossed[...]
+        for peer in space_peers:
+            to_total(peer, here).start()
+        for peer in space_peers:
+            to_total(peer, peer).wait_recv()
+        remote(totals, totals, last_send.at[0], last_recv.at[0], mem=own_end).start()
+        for peer in space_peers:
+            to_part(peer, here).wait_send()
+            to_total(peer, here).wait_send()
+        to_cross().wait_send()
+
+    pl.when(is_hub)(work)
+
+    @pl.when(is_end)
+    def _():
+        remote(totals, totals, last_send.at[0], last_recv.at[0], mem=own_hub).wait_recv()
+
+    prior_gram = totals[:, 0:members] / totals[:, members : members + 1]
+    prior[...] = prior_gram
+    carried = jnp.dot(
+        mixing_t, prior_gram, precision=HIGHEST, preferred_element_type=jnp.float32
+    )
+    posterior[...] = jnp.dot(
+        carried,
+        transform[...].astype(jnp.float32),
+        precision=HIGHEST,
+        preferred_element_type=jnp.float32,
+    )
+
+    @pl.when(is_hub)
+    def _():
+        remote(totals, totals, last_send.at[0], last_recv.at[0], mem=own_end).wait_send()
+        for piece in order:
+            raw(piece, me, 1 - side).wait_send()
+            forward(piece, own_end).wait_send()
+            to_beside(piece).wait_send()
+            to_far(piece).wait_send()
+            to_near(piece).wait_send()
+        for piece in order:
+            outward(1, piece, near_send, near_recv.at[piece], far_hub, 1 - side).wait_recv()
+
+    @pl.when(is_end)
+    def _():
+        for piece in order:
+            to_relay(piece).wait_send()
+            to_hub(piece).wait_send()
+        for piece in order:
+            for source in range(2):
+                from_side(piece, source).wait_recv()
+
+
+def hub_call(n_mem, n_space, pieces, ensemble, transform, obs_operator, obs_weight):
+    variables, local, cells = ensemble.shape
+    members = transform.shape[0]
+    n_obs = obs_operator.shape[0]
+    half = cells // 2
+    sizes = (n_mem, n_space, pieces, local, members, variables, n_obs, half)
+    vmem = pl.BlockSpec(memory_space=pltpu.VMEM)
+    any_space = pl.BlockSpec(memory_space=pl.ANY)
+    dma = pltpu.SemaphoreType.DMA
+    steps = len(pieces)
+    quarter = members // n_space
+    return pl.pallas_call(
+        functools.partial(hub_kernel, sizes),
+        out_shape=(
+            pltpu.VMEM((variables, local, cells), jnp.bfloat16),
+            pltpu.VMEM((members, members), jnp.float32),
+            pltpu.VMEM((members, members), jnp.float32),
+        ),
+        in_specs=[any_space] * 4,
+        out_specs=(vmem, vmem, vmem),
+        scratch_shapes=[
+            pltpu.VMEM(transform.shape, jnp.bfloat16),
+            pltpu.VMEM(obs_operator.shape, jnp.bfloat16),
+            pltpu.VMEM(obs_weight.shape, jnp.float32),
+            dma((3,)),
+            pltpu.VMEM((variables, members, half), jnp.bfloat16),
+            pltpu.VMEM((variables, local, half), jnp.bfloat16),
+            pltpu.VMEM((variables, members - local, half), jnp.bfloat16),
+            pltpu.VMEM((steps, n_obs * ROWS, PIECE * ROWS), jnp.bfloat16),
+            pltpu.VMEM((n_obs, members, half), jnp.float32),
+            pltpu.VMEM((members, LANES), jnp.float32),
+            pltpu.VMEM((n_space, quarter, LANES), jnp.float32),
+            pltpu.VMEM((quarter, LANES), jnp.float32),
+            pltpu.VMEM((quarter, LANES), jnp.float32),
+            pltpu.VMEM((members, LANES), jnp.float32),
+        ]
+        + [dma((steps,))] * 12
+        + [dma((steps, 2)), dma((steps,))]
+        + [dma((n_space,)), dma((n_space,)), dma((1,)), dma((1,))]
+        + [dma((n_space,)), dma((n_space,)), dma((1,)), dma((1,))]
+        + [pltpu.SemaphoreType.REGULAR, pltpu.SemaphoreType.REGULAR],
+        compiler_params=pltpu.CompilerParams(collective_id=0, has_side_effects=True),
+        name="hub_exchange",
+    )(ensemble, transform, obs_operator, obs_weight)
+
+
 def store(*refs):
     count = len(refs) // 2
     sources, targets, sems = refs[:count], refs[count : 2 * count], refs[-1]
@@ -327,6 +687,17 @@
     pieces = tuple(
         (start, min(PIECE, variables - start)) for start in range(0, variables, PIECE)
     )
+    if (
+        n_mem == 4
+        and local == ROWS
+        and members < LANES
+        and members % (8 * n_space) == 0
+        and cells % (2 * LANES) == 0
+    ):
+        by_variable, prior, posterior = write_out(*hub_call(
+            n_mem, n_space, pieces, jnp.transpose(ensemble, (1, 0, 2)), transform, obs_operator, obs_weight
+        ))
+        return jnp.transpose(by_variable, (1, 0, 2)), prior, posterior
     sizes = (n_mem, n_space, active, pieces, local, members, variables, n_obs, chunk)
     vmem = pl.BlockSpec(memory_space=pltpu.VMEM)
     any_space = pl.BlockSpec(memory_space=pl.ANY)
@@ -334,7 +705,7 @@
     slabs = (1, 1, ROWS, LANES) if local % ROWS == 0 else (n_mem, variables, local, chunk)
     dma = pltpu.SemaphoreType.DMA
     by_variable, prior, posterior = pl.pallas_call(
-        functools.partial(kernel, sizes),
+        functools.partial(line_kernel, sizes),
         out_shape=(
             pltpu.VMEM((variables, local, cells), jnp.bfloat16),
             pltpu.VMEM((members, members), jnp.float32),

time: 110 us -> 104 us (0.945); the launches traced: 109 us -> 104 us
  Pallas kernels: 108 us -> 104 us
    pallas_call x1, Pallas kernels: 107 us -> 102 us  [hub_call(): pl.pallas_call(functools.partial(hub_kernel, sizes), out_shape=(pltpu.VME...]
where the time goes in v1:
time: 104 us
  Pallas kernels  104 us (100%)
    pallas_call x1, Pallas kernels, hub_call(): pl.pallas_call(functools.partial(hub_kernel, sizes), out_shape=(pltpu.VME...  102 us

profile of v1, /device:TPU:10, one launch (start us, length us, event | category | flops | bytes accessed | tf_op | source)
XLA Modules:
  0.0 104.2 jit_solution(2687421158817330008)
XLA Ops:
  0.6 102.1 %hub_exchange.1 = (bf16[70,16,1024]{2,1,0:T(8,128)(2,1)S(1)}, f32[64,64]{1,0:T(8,128)S(1)}, f32[64,64]{1,0:T(8,128)S(1)}) custom-call(bf16[70,16,1024]{2,1,0:T(8,128)(2,1)} %bitcast.2, bf16[64,64]{1,0:T(8,128)(2,1)} %transform_in.1, bf16[16,70]{1,0:T(8,128)(2,1)} %operator_in.1, f32[16,1024]{1,0:T(8,128)} %weight_in.1), custom_call_target="tpu_custom_call" | custom-call | tf_op jit(solution)/shard_map/hub_exchange/pallas_call | solution.py:613
  102.8 1.5 %store_outputs.1 = (bf16[70,16,1024]{2,1,0:T(8,128)(2,1)}, f32[64,64]{1,0:T(8,128)}, f32[64,64]{1,0:T(8,128)}) custom-call(bf16[70,16,1024]{2,1,0:T(8,128)(2,1)S(1)} %get-tuple-element.9.refs_0_, f32[64,64]{1,0:T(8,128)S(1)} %get-tuple-element.10.refs_1_, f32[64,64]{1,0:T(8,128)S(1)} %get-tuple-element.11.refs_2_), custom_call_target="tpu_custom_call" | custom-call | tf_op jit(solution)/shard_map/store_outputs/pallas_call | solution.py:670

commit v2 on v1

--- a/solution.py
+++ b/solution.py
@@ -13,6 +13,7 @@
 PIECE = 14
 ROWS = 16
 LEAD = 2
+SENT, OUT, FINAL, PART, TOTAL, CROSS, LAST, SMALL = range(8)
 NT = (((1,), (1,)), ((), ()))
 
 
@@ -288,12 +289,8 @@
 
 def hub_kernel(
     sizes, ensemble, transform_in, operator_in, weight_in, analysis, prior, posterior,
-    transform, obs_operator, obs_weight, small_sem,
-    arrived, relay, results, observer, observed, gram, parts, summed, crossed, totals,
-    own_in, end_send, end_recv, relay_send, relay_recv, raw_send, raw_recv,
-    forward_send, forward_recv, beside_send, far_send, near_send, out_recv, near_recv,
-    part_send, part_recv, cross_send, cross_recv, total_send, total_recv, last_send, last_recv,
-    met, ready,
+    transform, obs_operator, obs_weight, arrived, relay, results, observer, observed,
+    gram, parts, summed, crossed, totals, sem, arrive, passing, met, ready,
 ):
     n_mem, n_space, pieces, local, members, variables, n_obs, half = sizes
     blocks = members // ROWS
@@ -331,60 +328,57 @@
         start, count = pieces[piece]
         return slice(start, start + count)
 
-    def raw(piece, rows_device, lanes_side):
+    def raw(piece, source, lanes_side):
         return remote(
             ensemble.at[span(piece), :, lanes_of(lanes_side)],
-            arrived.at[span(piece), rows_of(rows_device), :],
-            raw_send.at[piece], raw_recv.at[piece], mem=far_hub,
-        )
-
-    def forward(piece, rows_device):
+            arrived.at[span(piece), rows_of(source), :],
+            sem.at[SENT], arrive.at[piece], mem=far_hub,
+        )
+
+    def forward(piece, source):
         return remote(
-            relay.at[span(piece)], arrived.at[span(piece), rows_of(rows_device), :],
-            forward_send.at[piece], forward_recv.at[piece], mem=far_hub,
+            relay.at[span(piece)], arrived.at[span(piece), rows_of(source), :],
+            sem.at[SENT], arrive.at[piece], mem=far_hub,
         )
 
     def to_hub(piece):
         return remote(
             ensemble.at[span(piece), :, lanes_of(side)],
             arrived.at[span(piece), rows_of(own_end), :],
-            end_send.at[piece], end_recv.at[piece], mem=own_hub,
+            sem.at[SENT], arrive.at[piece], mem=own_hub,
         )
 
     def to_relay(piece):
         return remote(
             ensemble.at[span(piece), :, lanes_of(1 - side)], relay.at[span(piece)],
-            relay_send.at[piece], relay_recv.at[piece], mem=own_hub,
+            sem.at[SENT], passing.at[piece], mem=own_hub,
         )
 
     def own_raw(piece):
         return pltpu.make_async_copy(
             ensemble.at[span(piece), :, lanes_of(side)],
             arrived.at[span(piece), rows_of(me), :],
-            own_in.at[piece],
-        )
-
-    def outward(block, piece, send, recv, peer, columns):
+            arrive.at[piece],
+        )
+
+    def outward(block, piece, peer):
         return remote(
             results.at[span(piece), block * local : (block + 1) * local, :],
-            analysis.at[span(piece), :, lanes_of(columns)],
-            send.at[piece], recv, mem=peer,
-        )
-
-    def to_beside(piece):
-        return outward(0, piece, beside_send, out_recv.at[piece, side], own_end, side)
-
-    def to_near(piece):
-        return outward(1, piece, near_send, near_recv.at[piece], far_hub, side)
-
-    def to_far(piece):
-        return outward(2, piece, far_send, out_recv.at[piece, side], far_end, side)
-
-    def from_side(piece, source):
-        return outward(0, piece, beside_send, out_recv.at[piece, source], own_hub, source)
+            analysis.at[span(piece), :, lanes_of(side)],
+            sem.at[OUT], sem.at[FINAL], mem=peer,
+        )
+
+    def to_end():
+        return remote(totals, totals, sem.at[LAST], sem.at[CROSS], mem=own_end)
+
+    def landed(ref, semaphore):
+        remote(ref, ref, semaphore, semaphore, mem=far_hub).wait_recv()
+
+    def left(ref, semaphore):
+        remote(ref, ref, semaphore, semaphore, mem=far_hub).wait_send()
 
     loads = [
-        pltpu.make_async_copy(source, target, small_sem.at[index])
+        pltpu.make_async_copy(source, target, sem.at[SMALL + index])
         for index, (source, target) in enumerate(
             zip((transform_in, operator_in, weight_in), (transform, obs_operator, obs_weight))
         )
@@ -394,11 +388,11 @@
     @pl.when(is_hub)
     def _():
         signal(barrier, mem=far_hub)
-        signal(barrier, mem=own_end)
-        signal(barrier, mem=far_end)
         pl.semaphore_wait(barrier, 1)
         for piece in range(LEAD):
             raw(piece, me, 1 - side).start()
+        signal(barrier, mem=own_end)
+        signal(barrier, mem=far_end)
         for piece in order:
             own_raw(piece).start()
 
@@ -450,69 +444,76 @@
             observer[piece, :, 0:depth] = full.astype(jnp.bfloat16)
 
         def feed(piece):
-            to_relay(piece).wait_recv()
+            landed(relay.at[span(piece)], passing.at[piece])
             forward(piece, own_end).start()
             if piece + LEAD < len(pieces):
                 raw(piece + LEAD, me, 1 - side).start()
 
         def take(piece):
-            own_raw(piece).wait()
-            to_hub(piece).wait_recv()
-            raw(piece, far_hub, side).wait_recv()
-            forward(piece, far_end).wait_recv()
+            landed(arrived.at[span(piece)], arrive.at[piece])
 
         def mix(piece):
             start, count = pieces[piece]
-            for variable in range(start, start + count):
-                mixed = dot(mixer, arrived[variable])
-                mean = mixed[members : members + 1, :] / members
-                value = (mixed[:members, :] + keep * mean).astype(jnp.bfloat16)
-                analysis[variable, :, lanes_of(side)] = value[0:local, :]
-                results[variable] = value[local:, :]
+
+            def several(step, carry):
+                for offset in range(2):
+                    variable = start + step * 2 + offset
+                    mixed = dot(mixer, arrived[variable])
+                    mean = mixed[members : members + 1, :] / members
+                    value = (mixed[:members, :] + keep * mean).astype(jnp.bfloat16)
+                    analysis[variable, :, lanes_of(side)] = value[0:local, :]
+                    results[variable] = value[local:, :]
+                return carry
+
+            lax.fori_loop(0, count // 2, several, 0)
 
         def observe(piece):
             start, count = pieces[piece]
             depth = count * ROWS
-            for block in range(blocks):
-                at = slice(block * ROWS, (block + 1) * ROWS)
+            def one(block, carry):
+                at = pl.ds(pl.multiple_of(block * ROWS, ROWS), ROWS)
                 states = arrived[start : start + count, at, :].reshape(depth, half)
                 term = dot(observer[piece, :, 0:depth], states).reshape(n_obs, ROWS, half)
                 if piece == 0:
                     observed[:, at, :] = term
                 else:
                     observed[:, at, :] += term
+                return carry
+
+            lax.fori_loop(0, blocks, one, 0)
 
         def form_gram():
             weights = obs_weight[:, lanes_of(side)]
-            total = jnp.zeros((members, members), jnp.float32)
-            for quantity in range(n_obs):
+            def one(quantity, total):
                 values = observed[quantity]
                 departures = values - jnp.sum(values, axis=0, keepdims=True) / members
-                total += lax.dot_general(
-                    departures * weights[quantity : quantity + 1, :],
+                weight = obs_weight[pl.ds(quantity, 1), lanes_of(side)]
+                return total + lax.dot_general(
+                    departures * weight,
                     departures,
                     NT,
                     precision=HIGHEST,
                     preferred_element_type=jnp.float32,
                 )
+
+            total = lax.fori_loop(0, n_obs, one, jnp.zeros((members, members), jnp.float32))
             gram[...] = jnp.full(gram.shape, jnp.sum(weights), jnp.float32)
             gram[:, 0:members] = total
 
-        def to_part(peer, slot):
+        def to_part(peer):
             return remote(
-                gram.at[quarter_of(peer)], parts.at[slot],
-                part_send.at[peer], part_recv.at[slot], space=peer,
+                gram.at[quarter_of(peer)], parts.at[here],
+                sem.at[SMALL], sem.at[PART], space=peer,
             )
 
-        def to_cross():
-            return remote(summed, crossed, cross_send.at[0], cross_recv.at[0], mem=far_hub)
-
-        def to_total(peer, source):
+        def to_total(peer):
             return remote(
-                totals.at[quarter_of(source)], totals.at[quarter_of(source)],
-                total_send.at[peer], total_recv.at[source], space=peer,
+                totals.at[quarter_of(here)], totals.at[quarter_of(here)],
+                sem.at[SMALL + 1], sem.at[TOTAL], space=peer,
             )
 
+        to_cross = remote(summed, crossed, sem.at[SMALL + 2], sem.at[CROSS], mem=far_hub)
+        others = (n_space - 1) * quarter
         steps = len(pieces)
         for piece in range(min(LEAD, steps)):
             feed(piece)
@@ -522,48 +523,44 @@
         for piece in order:
             take(piece)
             mix(piece)
-            to_beside(piece).start()
+            outward(0, piece, own_end).start()
             behind.append(piece)
             if fed < steps:
                 feed(fed)
                 fed += 1
             if fed == steps:
                 for ahead in behind:
-                    to_far(ahead).start()
+                    outward(2, ahead, far_end).start()
                 behind = []
             observe(piece)
-        for piece in range(min(1, steps)):
-            to_near(piece).start()
+        outward(1, 0, far_hub).start()
         form_gram()
         for peer in space_peers:
-            to_part(peer, here).start()
+            to_part(peer).start()
         parts[here] = gram[quarter_of(here), :]
-        for peer in space_peers:
-            to_part(peer, peer).wait_recv()
+        landed(parts.at[0 : n_space - 1], sem.at[PART])
         total = parts[0]
         for slot in range(1, n_space):
             total += parts[slot]
         summed[...] = total
-        to_cross().start()
-        for piece in range(min(1, steps), steps):
-            to_near(piece).start()
-        to_cross().wait_recv()
+        to_cross.start()
+        for piece in order[1:]:
+            outward(1, piece, far_hub).start()
+        to_cross.wait_recv()
         totals[quarter_of(here), :] = total + crossed[...]
         for peer in space_peers:
-            to_total(peer, here).start()
-        for peer in space_peers:
-            to_total(peer, peer).wait_recv()
-        remote(totals, totals, last_send.at[0], last_recv.at[0], mem=own_end).start()
-        for peer in space_peers:
-            to_part(peer, here).wait_send()
-            to_total(peer, here).wait_send()
-        to_cross().wait_send()
+            to_total(peer).start()
+        landed(totals.at[0:others], sem.at[TOTAL])
+        to_end().start()
+        left(gram.at[0:others], sem.at[SMALL])
+        left(totals.at[0:others], sem.at[SMALL + 1])
+        to_cross.wait_send()
 
     pl.when(is_hub)(work)
 
     @pl.when(is_end)
     def _():
-        remote(totals, totals, last_send.at[0], last_recv.at[0], mem=own_hub).wait_recv()
+        to_end().wait_recv()
 
     prior_gram = totals[:, 0:members] / totals[:, members : members + 1]
     prior[...] = prior_gram
@@ -577,26 +574,17 @@
         preferred_element_type=jnp.float32,
     )
 
+    left(ensemble, sem.at[SENT])
+
     @pl.when(is_hub)
     def _():
-        remote(totals, totals, last_send.at[0], last_recv.at[0], mem=own_end).wait_send()
-        for piece in order:
-            raw(piece, me, 1 - side).wait_send()
-            forward(piece, own_end).wait_send()
-            to_beside(piece).wait_send()
-            to_far(piece).wait_send()
-            to_near(piece).wait_send()
-        for piece in order:
-            outward(1, piece, near_send, near_recv.at[piece], far_hub, 1 - side).wait_recv()
+        to_end().wait_send()
+        left(results, sem.at[OUT])
+        landed(analysis.at[:, :, lanes_of(1 - side)], sem.at[FINAL])
 
     @pl.when(is_end)
     def _():
-        for piece in order:
-            to_relay(piece).wait_send()
-            to_hub(piece).wait_send()
-        for piece in order:
-            for source in range(2):
-                from_side(piece, source).wait_recv()
+        landed(analysis, sem.at[FINAL])
 
 
 def hub_call(n_mem, n_space, pieces, ensemble, transform, obs_operator, obs_weight):
@@ -623,7 +611,6 @@
             pltpu.VMEM(transform.shape, jnp.bfloat16),
             pltpu.VMEM(obs_operator.shape, jnp.bfloat16),
             pltpu.VMEM(obs_weight.shape, jnp.float32),
-            dma((3,)),
             pltpu.VMEM((variables, members, half), jnp.bfloat16),
             pltpu.VMEM((variables, local, half), jnp.bfloat16),
             pltpu.VMEM((variables, members - local, half), jnp.bfloat16),
@@ -634,12 +621,12 @@
             pltpu.VMEM((quarter, LANES), jnp.float32),
             pltpu.VMEM((quarter, LANES), jnp.float32),
             pltpu.VMEM((members, LANES), jnp.float32),
-        ]
-        + [dma((steps,))] * 12
-        + [dma((steps, 2)), dma((steps,))]
-        + [dma((n_space,)), dma((n_space,)), dma((1,)), dma((1,))]
-        + [dma((n_space,)), dma((n_space,)), dma((1,)), dma((1,))]
-        + [pltpu.SemaphoreType.REGULAR, pltpu.SemaphoreType.REGULAR],
+            dma((SMALL + 3,)),
+            dma((steps,)),
+            dma((steps,)),
+            pltpu.SemaphoreType.REGULAR,
+            pltpu.SemaphoreType.REGULAR,
+        ],
         compiler_params=pltpu.CompilerParams(collective_id=0, has_side_effects=True),
         name="hub_exchange",
     )(ensemble, transform, obs_operator, obs_weight)
@@ -648,17 +635,9 @@
 def store(*refs):
     count = len(refs) // 2
     sources, targets, sems = refs[:count], refs[count : 2 * count], refs[-1]
-    pairs = []
-    for source, target in zip(sources, targets):
-        if len(source.shape) == 3:
-            for start in range(0, source.shape[0], PIECE):
-                part = slice(start, min(start + PIECE, source.shape[0]))
-                pairs.append((source.at[part], target.at[part]))
-        else:
-            pairs.append((source, target))
     copies = [
         pltpu.make_async_copy(source, target, sems.at[index])
-        for index, (source, target) in enumerate(pairs)
+        for index, (source, target) in enumerate(zip(sources, targets))
     ]
     for copy in copies:
         copy.start()
@@ -672,7 +651,7 @@
         out_shape=tuple(jax.ShapeDtypeStruct(a.shape, a.dtype) for a in arrays),
         in_specs=[pl.BlockSpec(memory_space=pl.ANY)] * len(arrays),
         out_specs=tuple([pl.BlockSpec(memory_space=pl.ANY)] * len(arrays)),
-        scratch_shapes=[pltpu.SemaphoreType.DMA((len(arrays) + pl.cdiv(arrays[0].shape[0], PIECE),))],
+        scratch_shapes=[pltpu.SemaphoreType.DMA((len(arrays),))],
         compiler_params=pltpu.CompilerParams(vmem_limit_bytes=8 << 20),
         name="store_outputs",
     )(*arrays)

time: 104 us -> 104 us (level)
  no operation moved by 1% of the time
where the time goes in v2:
time: 104 us; the launch traced here: 103 us
  Pallas kernels  103 us (99%)
    pallas_call x1, Pallas kernels, hub_call(): pl.pallas_call(functools.partial(hub_kernel, sizes), out_shape=(pltpu.VME...  101 us

profile of v2, /device:TPU:10, one launch (start us, length us, event | category | flops | bytes accessed | tf_op | source)
XLA Modules:
  0.0 103.5 jit_solution(12697340679401160548)
XLA Ops:
  0.6 101.4 %hub_exchange.1 = (bf16[70,16,1024]{2,1,0:T(8,128)(2,1)S(1)}, f32[64,64]{1,0:T(8,128)S(1)}, f32[64,64]{1,0:T(8,128)S(1)}) custom-call(bf16[70,16,1024]{2,1,0:T(8,128)(2,1)} %bitcast.2, bf16[64,64]{1,0:T(8,128)(2,1)} %transform_in.1, bf16[16,70]{1,0:T(8,128)(2,1)} %operator_in.1, f32[16,1024]{1,0:T(8,128)} %weight_in.1), custom_call_target="tpu_custom_call" | custom-call | tf_op jit(solution)/shard_map/hub_exchange/pallas_call | solution.py:601
  102.1 1.4 %store_outputs.1 = (bf16[70,16,1024]{2,1,0:T(8,128)(2,1)}, f32[64,64]{1,0:T(8,128)}, f32[64,64]{1,0:T(8,128)}) custom-call(bf16[70,16,1024]{2,1,0:T(8,128)(2,1)S(1)} %get-tuple-element.9.refs_0_, f32[64,64]{1,0:T(8,128)S(1)} %get-tuple-element.10.refs_1_, f32[64,64]{1,0:T(8,128)S(1)} %get-tuple-element.11.refs_2_), custom_call_target="tpu_custom_call" | custom-call | tf_op jit(solution)/shard_map/store_outputs/pallas_call | solution.py:649

commit v3 on v2

--- a/solution.py
+++ b/solution.py
@@ -13,7 +13,7 @@
 PIECE = 14
 ROWS = 16
 LEAD = 2
-SENT, OUT, FINAL, PART, TOTAL, CROSS, LAST, SMALL = range(8)
+SENT, OUT, LAST, SMALL, FINAL, PART, TOTAL, CROSS = range(8)
 NT = (((1,), (1,)), ((), ()))
 
 
@@ -290,7 +290,7 @@
 def hub_kernel(
     sizes, ensemble, transform_in, operator_in, weight_in, analysis, prior, posterior,
     transform, obs_operator, obs_weight, arrived, relay, results, observer, observed,
-    gram, parts, summed, crossed, totals, sem, arrive, passing, met, ready,
+    gram, parts, summed, crossed, totals, sem, arrive, passing, ready,
 ):
     n_mem, n_space, pieces, local, members, variables, n_obs, half = sizes
     blocks = members // ROWS
@@ -362,9 +362,10 @@
         )
 
     def outward(block, piece, peer):
+        rows = span(piece)
         return remote(
-            results.at[span(piece), block * local : (block + 1) * local, :],
-            analysis.at[span(piece), :, lanes_of(side)],
+            results.at[rows, block * local : (block + 1) * local, :],
+            analysis.at[rows, :, lanes_of(side)],
             sem.at[OUT], sem.at[FINAL], mem=peer,
         )
 
@@ -378,9 +379,11 @@
         remote(ref, ref, semaphore, semaphore, mem=far_hub).wait_send()
 
     loads = [
-        pltpu.make_async_copy(source, target, sem.at[SMALL + index])
-        for index, (source, target) in enumerate(
-            zip((transform_in, operator_in, weight_in), (transform, obs_operator, obs_weight))
+        pltpu.make_async_copy(source, target, sem.at[index])
+        for index, source, target in zip(
+            (OUT, LAST, SMALL),
+            (transform_in, operator_in, weight_in),
+            (transform, obs_operator, obs_weight),
         )
     ]
     barrier = pltpu.get_barrier_semaphore()
@@ -407,8 +410,8 @@
                 to_relay(piece + 1).start()
             to_hub(piece).start()
         for peer in space_peers:
-            signal(met, space=peer)
-        pl.semaphore_wait(met, n_space - 1)
+            signal(ready, space=peer)
+        pl.semaphore_wait(ready, n_space - 1)
         signal(ready, mem=own_hub)
         signal(ready, mem=far_hub)
 
@@ -483,7 +486,6 @@
             lax.fori_loop(0, blocks, one, 0)
 
         def form_gram():
-            weights = obs_weight[:, lanes_of(side)]
             def one(quantity, total):
                 values = observed[quantity]
                 departures = values - jnp.sum(values, axis=0, keepdims=True) / members
@@ -497,7 +499,7 @@
                 )
 
             total = lax.fori_loop(0, n_obs, one, jnp.zeros((members, members), jnp.float32))
-            gram[...] = jnp.full(gram.shape, jnp.sum(weights), jnp.float32)
+            gram[...] = jnp.full(gram.shape, jnp.sum(obs_weight[...]), jnp.float32)
             gram[:, 0:members] = total
 
         def to_part(peer):
@@ -509,10 +511,10 @@
         def to_total(peer):
             return remote(
                 totals.at[quarter_of(here)], totals.at[quarter_of(here)],
-                sem.at[SMALL + 1], sem.at[TOTAL], space=peer,
+                sem.at[LAST], sem.at[TOTAL], space=peer,
             )
 
-        to_cross = remote(summed, crossed, sem.at[SMALL + 2], sem.at[CROSS], mem=far_hub)
+        to_cross = remote(summed, crossed, sem.at[SMALL], sem.at[CROSS], mem=far_hub)
         others = (n_space - 1) * quarter
         steps = len(pieces)
         for piece in range(min(LEAD, steps)):
@@ -542,19 +544,25 @@
         total = parts[0]
         for slot in range(1, n_space):
             total += parts[slot]
-        summed[...] = total
+        upper = quarter // 2
+        summed[:, 0:members] = total[0:upper, 0:members]
+        summed[:, members : 2 * members] = total[upper:, 0:members]
+        left(gram.at[0:others], sem.at[SMALL])
         to_cross.start()
         for piece in order[1:]:
             outward(1, piece, far_hub).start()
         to_cross.wait_recv()
-        totals[quarter_of(here), :] = total + crossed[...]
+        totals[quarter_of(here), members:] = total[:, members:]
+        whole = summed[...] + crossed[...]
+        for part in range(2):
+            rows = pl.ds(pl.multiple_of(here * quarter + part * upper, upper), upper)
+            totals[rows, 0:members] = whole[:, part * members : (part + 1) * members]
+        to_cross.wait_send()
         for peer in space_peers:
             to_total(peer).start()
         landed(totals.at[0:others], sem.at[TOTAL])
+        left(totals.at[0:others], sem.at[LAST])
         to_end().start()
-        left(gram.at[0:others], sem.at[SMALL])
-        left(totals.at[0:others], sem.at[SMALL + 1])
-        to_cross.wait_send()
 
     pl.when(is_hub)(work)
 
@@ -618,13 +626,12 @@
             pltpu.VMEM((n_obs, members, half), jnp.float32),
             pltpu.VMEM((members, LANES), jnp.float32),
             pltpu.VMEM((n_space, quarter, LANES), jnp.float32),
-            pltpu.VMEM((quarter, LANES), jnp.float32),
-            pltpu.VMEM((quarter, LANES), jnp.float32),
+            pltpu.VMEM((quarter // 2, LANES), jnp.float32),
+            pltpu.VMEM((quarter // 2, LANES), jnp.float32),
             pltpu.VMEM((members, LANES), jnp.float32),
-            dma((SMALL + 3,)),
+            dma((CROSS + 1,)),
             dma((steps,)),
             dma((steps,)),
-            pltpu.SemaphoreType.REGULAR,
             pltpu.SemaphoreType.REGULAR,
         ],
         compiler_params=pltpu.CompilerParams(collective_id=0, has_side_effects=True),
@@ -669,8 +676,8 @@
     if (
         n_mem == 4
         and local == ROWS
-        and members < LANES
-        and members % (8 * n_space) == 0
+        and 2 * members == LANES
+        and members % (16 * n_space) == 0
         and cells % (2 * LANES) == 0
     ):
         by_variable, prior, posterior = write_out(*hub_call(

time: 104 us -> 104 us (level)
  no operation moved by 1% of the time
where the time goes in v3:
time: 104 us; the launch traced here: 103 us
  Pallas kernels  103 us (99%)
    pallas_call x1, Pallas kernels, hub_call(): pl.pallas_call(functools.partial(hub_kernel, sizes), out_shape=(pltpu.VME...  101 us

profile of v3, /device:TPU:10, one launch (start us, length us, event | category | flops | bytes accessed | tf_op | source)
XLA Modules:
  0.0 103.4 jit_solution(10464519184446039164)
XLA Ops:
  0.6 101.3 %hub_exchange.1 = (bf16[70,16,1024]{2,1,0:T(8,128)(2,1)S(1)}, f32[64,64]{1,0:T(8,128)S(1)}, f32[64,64]{1,0:T(8,128)S(1)}) custom-call(bf16[70,16,1024]{2,1,0:T(8,128)(2,1)} %bitcast.2, bf16[64,64]{1,0:T(8,128)(2,1)} %transform_in.1, bf16[16,70]{1,0:T(8,128)(2,1)} %operator_in.1, f32[16,1024]{1,0:T(8,128)} %weight_in.1), custom_call_target="tpu_custom_call" | custom-call | tf_op jit(solution)/shard_map/hub_exchange/pallas_call | solution.py:609
  101.9 1.4 %store_outputs.1 = (bf16[70,16,1024]{2,1,0:T(8,128)(2,1)}, f32[64,64]{1,0:T(8,128)}, f32[64,64]{1,0:T(8,128)}) custom-call(bf16[70,16,1024]{2,1,0:T(8,128)(2,1)S(1)} %get-tuple-element.9.refs_0_, f32[64,64]{1,0:T(8,128)S(1)} %get-tuple-element.10.refs_1_, f32[64,64]{1,0:T(8,128)S(1)} %get-tuple-element.11.refs_2_), custom_call_target="tpu_custom_call" | custom-call | tf_op jit(solution)/shard_map/store_outputs/pallas_call | solution.py:656
